TPU v7x, 32 devices: a whole 2x2x4 slice. The times are simulated.
32 devices in a mesh: col: 8 (over z, y), row: 4 (over x, core).
Axes of the slice: x: 2, y: 2, z: 4, core: 2. Of those that a mesh axis runs over, the one named last changes fastest.
Arguments:
- hyper_params: float32 [3], replicated
- w_in: float32 [4, 1024, 16384], P(None, 'row', 'col')
- x_in: bfloat16 [4, 1024, 1024], P(None, None, 'row')
- dy_in: bfloat16 [4, 1024, 16384], P(None, None, 'col')
- row_in: float32 [4, 1024], P(None, 'row')
- col_in: float32 [4, 16384], P(None, 'col')
- w_out: float32 [4, 16384, 1024], P(None, 'col', 'row')
- x_out: bfloat16 [4, 1024, 16384], P(None, None, 'col')
- dy_out: bfloat16 [4, 1024, 1024], P(None, None, 'row')
- row_out: float32 [4, 16384], P(None, 'col')
- col_out: float32 [4, 1024], P(None, 'row')
Outputs:
- output 1: float32 [4, 1024, 16384], P(None, 'row', 'col')
- output 2: float32 [4, 1024], P(None, 'row')
- output 3: float32 [4, 16384], P(None, 'col')
- output 4: float32 [4, 16384, 1024], P(None, 'col', 'row')
- output 5: float32 [4, 16384], P(None, 'col')
- output 6: float32 [4, 1024], P(None, 'row')
All inputs are finite; a program needn't handle non-finite values.
Results may differ from a plain program's by a relative error of at most 0.001.
Values are sent between devices in bfloat16 or wider.
A program may use at most 1 GiB of HBM per device.

v0:
```python
import jax
import jax.numpy as jnp
from jax import lax
from jax.sharding import PartitionSpec as P

EPS_ONE = 1e-30
EPS_TWO = 1e-3
BOTH_AXES = ('col', 'row')


def update_block(w_blk, x_blk, dy_blk, row_old, col_old, hyper_params, rows_axis, cols_axis, n_rows, n_cols):
    beta_two = hyper_params[0]
    rho_step = hyper_params[1]
    clip_max = hyper_params[2]
    n_total = float(n_rows * n_cols)
    grad_blk = lax.dot_general(x_blk, dy_blk, (((0,), (0,)), ((), ())), preferred_element_type=jnp.float32)
    sq_grad = grad_blk * grad_blk + EPS_ONE
    row_part = jnp.sum(sq_grad, axis=1)
    col_part = jnp.sum(sq_grad, axis=0)
    lead_col = (lax.axis_index(cols_axis) == 0).astype(jnp.float32)
    scalars = jnp.stack([jnp.sum(row_part), jnp.sum(w_blk * w_blk), lead_col * jnp.sum(row_old)])
    row_sum = lax.psum(row_part, cols_axis)
    col_sum = lax.psum(col_part, rows_axis)
    scalar_sum = lax.psum(scalars, BOTH_AXES)
    row_new = beta_two * row_old + (1.0 - beta_two) * (row_sum / n_cols)
    col_new = beta_two * col_old + (1.0 - beta_two) * (col_sum / n_rows)
    row_mean = beta_two * (scalar_sum[2] / n_rows) + (1.0 - beta_two) * (scalar_sum[0] / n_total)
    update = grad_blk * lax.rsqrt((row_new / row_mean)[:, None] * col_new[None, :])
    upd_sq = lax.psum(jnp.sum(update * update), BOTH_AXES)
    upd_rms = jnp.sqrt(upd_sq / n_total)
    w_rms = jnp.sqrt(scalar_sum[1] / n_total)
    step_size = rho_step * jnp.maximum(EPS_TWO, w_rms) / jnp.maximum(1.0, upd_rms / clip_max)
    return w_blk - step_size * update, row_new, col_new


def solution(mesh):
    n_col = mesh.shape['col']
    n_row = mesh.shape['row']
    tile_in = P(None, 'row', 'col')
    tile_out = P(None, 'col', 'row')
    lane_row = P(None, None, 'row')
    lane_col = P(None, None, 'col')
    vec_row = P(None, 'row')
    vec_col = P(None, 'col')

    def local_step(hyper_params, w_in, x_in, dy_in, row_in, col_in, w_out, x_out, dy_out, row_out, col_out):
        d_model = w_in.shape[1] * n_row
        d_hidden = w_in.shape[2] * n_col
        results = []
        for layer_idx in range(w_in.shape[0]):
            in_result = update_block(w_in[layer_idx], x_in[layer_idx], dy_in[layer_idx], row_in[layer_idx], col_in[layer_idx], hyper_params, 'row', 'col', d_model, d_hidden)
            out_result = update_block(w_out[layer_idx], x_out[layer_idx], dy_out[layer_idx], row_out[layer_idx], col_out[layer_idx], hyper_params, 'col', 'row', d_hidden, d_model)
            results.append(in_result + out_result)
        return tuple(jnp.stack([res_item[out_idx] for res_item in results]) for out_idx in range(6))

    return jax.shard_map(local_step, mesh=mesh, in_specs=(P(), tile_in, lane_row, lane_col, vec_row, vec_col, tile_out, lane_col, lane_row, vec_col, vec_row), out_specs=(tile_in, vec_row, vec_col, tile_out, vec_col, vec_row), check_vma=False)
```

profile of v0, /device:TPU:0, one launch (start us, length us, event | category | flops | bytes accessed | tf_op | source)
XLA Modules:
  0.0 264.6 jit_solution(16149925941648885384)
XLA Ops:
  7.2 4.9 %fusion.44 = (f32[256]{0:T(256)S(1)}, f32[2048]{0:T(1024)}, f32[]{:T(128)}, f32[256,2048]{1,0:T(8,128)S(1)}) fusion(bf16[4,1024,2048]{2,1,0:T(8,128)(2,1)} %param.14, bf16[4,1024,256]{2,1,0:T(8,128)(2,1)} %param.13), kind=kOutput, calls=%fused_computation.86 | convolution fusion | flops 1076360960 | bytes 6824964 | tf_op jit(solution)/shard_map/dot_general | solution.py:16
  12.1 6.5 %fusion.41 = (f32[256]{0:T(256)S(1)}, f32[2048]{0:T(1024)}, f32[]{:T(128)}, f32[256,2048]{1,0:T(8,128)}) fusion(bf16[4,1024,2048]{2,1,0:T(8,128)(2,1)} %param.14, bf16[4,1024,256]{2,1,0:T(8,128)(2,1)} %param.13), kind=kOutput, calls=%fused_computation.83 | convolution fusion | flops 1076360960 | bytes 6824964 | tf_op jit(solution)/shard_map/dot_general | solution.py:16
  18.6 3.4 %fusion.50 = (f32[256]{0:T(256)S(1)}, f32[2048]{0:T(1024)}, f32[]{:T(128)}, f32[256,2048]{1,0:T(8,128)}) fusion(bf16[4,1024,2048]{2,1,0:T(8,128)(2,1)S(1)} %copy-done.18, bf16[4,1024,256]{2,1,0:T(8,128)(2,1)S(1)} %copy-done.20), kind=kOutput, calls=%fused_computation.92 | convolution fusion | flops 1076360960 | bytes 6824964 | tf_op jit(solution)/shard_map/dot_general | solution.py:16
  22.0 3.4 %fusion.47 = (f32[256]{0:T(256)S(1)}, f32[2048]{0:T(1024)}, f32[]{:T(128)}, f32[256,2048]{1,0:T(8,128)}) fusion(bf16[4,1024,2048]{2,1,0:T(8,128)(2,1)S(1)} %copy-done.18, bf16[4,1024,256]{2,1,0:T(8,128)(2,1)S(1)} %copy-done.20), kind=kOutput, calls=%fused_computation.89 | convolution fusion | flops 1076360960 | bytes 6824964 | tf_op jit(solution)/shard_map/dot_general | solution.py:16
  26.7 3.5 %fusion.56 = (f32[2048]{0:T(1024)}, f32[256]{0:T(256)S(1)}, f32[]{:T(128)}, f32[2048,256]{1,0:T(8,128)}) fusion(bf16[4,1024,256]{2,1,0:T(8,128)(2,1)S(1)} %copy-done.21, bf16[4,1024,2048]{2,1,0:T(8,128)(2,1)S(1)} %copy-done.19), kind=kOutput, calls=%fused_computation.98 | convolution fusion | flops 1076360960 | bytes 6824964 | tf_op jit(solution)/shard_map/dot_general | solution.py:16
  30.2 3.5 %fusion.53 = (f32[2048]{0:T(1024)}, f32[256]{0:T(256)S(1)}, f32[]{:T(128)}, f32[2048,256]{1,0:T(8,128)}) fusion(bf16[4,1024,256]{2,1,0:T(8,128)(2,1)S(1)} %copy-done.21, bf16[4,1024,2048]{2,1,0:T(8,128)(2,1)S(1)} %copy-done.19), kind=kOutput, calls=%fused_computation.95 | convolution fusion | flops 1076360960 | bytes 6824964 | tf_op jit(solution)/shard_map/dot_general | solution.py:16
  33.7 3.6 %fusion.62 = (f32[2048]{0:T(1024)}, f32[256]{0:T(256)S(1)}, f32[]{:T(128)}, f32[2048,256]{1,0:T(8,128)}) fusion(bf16[4,1024,256]{2,1,0:T(8,128)(2,1)S(1)} %copy-done.21, bf16[4,1024,2048]{2,1,0:T(8,128)(2,1)S(1)} %copy-done.19), kind=kOutput, calls=%fused_computation.104 | convolution fusion | flops 1076360960 | bytes 6824964 | tf_op jit(solution)/shard_map/dot_general | solution.py:16
  37.3 3.8 %fusion.59 = (f32[2048]{0:T(1024)}, f32[256]{0:T(256)S(1)}, f32[]{:T(128)}, f32[2048,256]{1,0:T(8,128)}) fusion(bf16[4,1024,256]{2,1,0:T(8,128)(2,1)S(1)} %copy-done.21, bf16[4,1024,2048]{2,1,0:T(8,128)(2,1)S(1)} %copy-done.19), kind=kOutput, calls=%fused_computation.101 | convolution fusion | flops 1076360960 | bytes 6824964 | tf_op jit(solution)/shard_map/dot_general | solution.py:16
  41.8 5.0 %fusion.38 = (f32[]{:T(128)}, f32[]{:T(128)}, f32[]{:T(128)}, f32[]{:T(128)}) fusion(f32[4,256,2048]{2,1,0:T(8,128)} %param.12), kind=kLoop, calls=%fused_computation.56 | loop fusion | flops 4194300 | bytes 8388624 | tf_op jit(solution)/shard_map/reduce_sum | solution.py:21
  46.8 4.7 %fusion.30 = (f32[]{:T(128)}, f32[]{:T(128)}, f32[]{:T(128)}, f32[]{:T(128)}) fusion(f32[4,2048,256]{2,1,0:T(8,128)} %param.17), kind=kLoop, calls=%fused_computation.40 | loop fusion | flops 4194300 | bytes 8388624 | tf_op jit(solution)/shard_map/reduce_sum | solution.py:21
  70.3 42.0 %all-reduce.1 = (f32[3]{0:T(128)S(1)}, f32[3]{0:T(128)S(1)}, f32[3]{0:T(128)S(1)}, f32[3]{0:T(128)S(1)}, f32[3]{0:T(128)S(1)}, /*index=5*/f32[3]{0:T(128)S(1)}, f32[3]{0:T(128)S(1)}, f32[3]{0:T(128)S(1)}) all-reduce(f32[3]{0:T(128)S(1)} %pad_maximum_fusion.9, ...), channel_id=1, replica_groups=mesh['col'=8,'row'=4] {'col','row'}, use_global_device_ids=true, to_apply=%region_33.0 | all-reduce | flops 24 | bytes 192 | tf_op jit(solution)/shard_map/psum | solution.py:24
  125.2 21.3 %all-reduce.2 = (f32[256]{0:T(256)S(1)}, f32[256]{0:T(256)S(1)}, f32[256]{0:T(256)S(1)}, f32[256]{0:T(256)S(1)}, f32[256]{0:T(256)S(1)}, /*index=5*/f32[256]{0:T(256)S(1)}, f32[256]{0:T(256)S(1)}, f32[256]{0:T(256)S(1)}) all-reduce(f32[256]{0:T(256)S(1)} %get-tuple-element.35, ...), channel_id=1, replica_groups=mesh['col'=8,'row'=4] {'col'}, use_global_device_ids=true, to_apply=%region_35.0 | all-reduce | flops 2048 | bytes 16384 | tf_op jit(solution)/shard_map/psum | solution.py:22
  168.8 3.0 %multiply_reduce_fusion = f32[]{:T(128)} fusion(f32[2048,256]{1,0:T(8,128)} %get-tuple-element.155, f32[256]{0:T(256)S(1)} %multiply_add_fusion.16, f32[2048]{0:T(1024)S(1)} %get-tuple-element.84), kind=kLoop, calls=%fused_computation.58 | loop fusion | flops 2097151 | bytes 2106372 | tf_op jit(solution)/shard_map/reduce_sum | solution.py:29
  175.8 1.7 multiply_reduce_fusion.4
  177.5 1.7 multiply_reduce_fusion.5
  179.2 1.7 multiply_reduce_fusion.6
  180.9 1.7 multiply_reduce_fusion.7
  183.2 37.7 %all-reduce = (f32[]{:T(128)}, f32[]{:T(128)}, f32[]{:T(128)}, f32[]{:T(128)}, f32[]{:T(128)}, /*index=5*/f32[]{:T(128)}, f32[]{:T(128)}, f32[]{:T(128)}) all-reduce(f32[]{:T(128)} %multiply_reduce_fusion.4, f32[]{:T(128)} %multiply_reduce_fusion.5, f32[]{:T(128)} %multiply_reduce_fusion.6, ...), channel_id=1, replica_groups=mesh['col'=8,'row'=4] {'col','row'}, use_global_device_ids=true, to_apply=%region_39.0 | all-reduce | flops 8 | bytes 64 | tf_op jit(solution)/shard_map/psum | solution.py:29
  231.1 3.9 %fusion.27 = f32[1,2048,256]{2,1,0:T(8,128)} fusion(f32[4,2048,256]{2,1,0:T(8,128)} %param.17, f32[2048,256]{1,0:T(8,128)} %get-tuple-element.156, f32[]{:T(128)S(6)} %div.309, f32[256]{0:T(256)S(1)} %multiply_add_fusion.17, f32[2048]{0:T(1024)S(1)} %get-tuple-element.82), kind=kLoop, calls=%fused_computation.33 | loop fusion | flops 2097152 | bytes 6300676 | tf_op jit(solution)/shard_map/stack | solution.py:54
  235.1 4.0 %fusion.35 = f32[1,256,2048]{2,1,0:T(8,128)} fusion(f32[4,256,2048]{2,1,0:T(8,128)} %param.12, f32[256,2048]{1,0:T(8,128)} %get-tuple-element.152, f32[]{:T(128)S(6)} %div.269, f32[2048]{0:T(1024)S(1)} %multiply_add_fusion.13, f32[256]{0:T(256)S(1)} %get-tuple-element.90), kind=kLoop, calls=%fused_computation.49 | loop fusion | flops 2097152 | bytes 6300676 | tf_op jit(solution)/shard_map/stack | solution.py:54
  239.4 5.4 %fusion.31 = (f32[1,2048,256]{2,1,0:T(8,128)S(1)}, f32[1,2048,256]{2,1,0:T(8,128)S(1)}, f32[1,2048,256]{2,1,0:T(8,128)S(1)}) fusion(f32[4,2048,256]{2,1,0:T(8,128)} %param.17, f32[2048,256]{1,0:T(8,128)} %get-tuple-element.158, f32[]{:T(128)S(6)} %div.289, f32[256]{0:T(256)S(1)} %multiply_add_fusion.19, f32[2048]{0:T(1024)S(1)} %get-tuple-element.78, ...), kind=kLoop, calls=%fused_computation.41 | loop fusion | flops 6291456 | bytes 18902028 | tf_op jit(solution)/shard_map/stack | solution.py:54
  245.3 3.8 %fusion.39 = (f32[1,256,2048]{2,1,0:T(8,128)S(1)}, f32[1,256,2048]{2,1,0:T(8,128)S(1)}, f32[1,256,2048]{2,1,0:T(8,128)S(1)}) fusion(f32[4,256,2048]{2,1,0:T(8,128)} %param.12, f32[256,2048]{1,0:T(8,128)S(1)} %copy-done.1, f32[]{:T(128)S(6)} %div.249, f32[2048]{0:T(1024)S(1)} %multiply_add_fusion.15, f32[256]{0:T(256)S(1)} %get-tuple-element.86, ...), kind=kLoop, calls=%fused_computation.57 | loop fusion | flops 6291456 | bytes 18902028 | tf_op jit(solution)/shard_map/stack | solution.py:54
  249.8 3.7 %pad_maximum_fusion = f32[4,256,2048]{2,1,0:T(8,128)} fusion(f32[1,256,2048]{2,1,0:T(8,128)S(1)} %get-tuple-element.98, f32[1,256,2048]{2,1,0:T(8,128)S(1)} %copy-done.9, f32[1,256,2048]{2,1,0:T(8,128)S(1)} %get-tuple-element.99, f32[1,256,2048]{2,1,0:T(8,128)S(1)} %get-tuple-element.97), kind=kLoop, calls=%fused_computation | loop fusion | flops 6291456 | bytes 16777216 | tf_op jit(solution)/shard_map/stack | solution.py:54
  253.4 3.7 %pad_maximum_fusion.1 = f32[4,2048,256]{2,1,0:T(8,128)} fusion(f32[1,2048,256]{2,1,0:T(8,128)S(1)} %get-tuple-element.95, f32[1,2048,256]{2,1,0:T(8,128)S(1)} %copy-done.8, f32[1,2048,256]{2,1,0:T(8,128)S(1)} %get-tuple-element.96, f32[1,2048,256]{2,1,0:T(8,128)S(1)} %get-tuple-element.94), kind=kLoop, calls=%fused_computation.1 | loop fusion | flops 6291456 | bytes 16777216 | tf_op jit(solution)/shard_map/stack | solution.py:54
  (89 shorter events, 31.0 us)
Async XLA Ops:
  7.2 158.0 %all-reduce.6.cloned.1.call-start = ((), (), s32[]{:S(2)}) async-start(), calls=%async_computation | async-start | bytes 131072 | tf_op jit(solution)/shard_map/psum | solution.py:23
  7.2 11.4 %copy-start.18 = (bf16[4,1024,2048]{2,1,0:T(8,128)(2,1)S(1)}, bf16[4,1024,2048]{2,1,0:T(8,128)(2,1)}, u32[]{:S(2)}) copy-start(bf16[4,1024,2048]{2,1,0:T(8,128)(2,1)} %param.14) | copy-start | bytes 50331652
  12.1 6.5 %copy-start.20 = (bf16[4,1024,256]{2,1,0:T(8,128)(2,1)S(1)}, bf16[4,1024,256]{2,1,0:T(8,128)(2,1)}, u32[]{:S(2)}) copy-start(bf16[4,1024,256]{2,1,0:T(8,128)(2,1)} %param.13) | copy-start | bytes 6291460
  18.6 7.3 %copy-start.19 = (bf16[4,1024,2048]{2,1,0:T(8,128)(2,1)S(1)}, bf16[4,1024,2048]{2,1,0:T(8,128)(2,1)}, u32[]{:S(2)}) copy-start(bf16[4,1024,2048]{2,1,0:T(8,128)(2,1)} %param.18) | copy-start | bytes 50331652
  22.0 4.7 %copy-start.21 = (bf16[4,1024,256]{2,1,0:T(8,128)(2,1)S(1)}, bf16[4,1024,256]{2,1,0:T(8,128)(2,1)}, u32[]{:S(2)}) copy-start(bf16[4,1024,256]{2,1,0:T(8,128)(2,1)} %param.19) | copy-start | bytes 6291460
  37.3 3.8 %copy-start.15 = (f32[3]{0:T(128)S(1)}, f32[3]{0:T(128)}, u32[]{:S(2)}) copy-start(f32[3]{0:T(128)} %param.11) | copy-start | bytes 40
  46.7 4.7 %copy-start.16 = (f32[4,256]{1,0:T(4,128)S(1)}, f32[4,256]{1,0:T(4,128)}, u32[]{:S(2)}) copy-start(f32[4,256]{1,0:T(4,128)} %param.21) | copy-start | bytes 12292
  46.7 4.7 %copy-start.17 = (f32[4,256]{1,0:T(4,128)S(1)}, f32[4,256]{1,0:T(4,128)}, u32[]{:S(2)}) copy-start(f32[4,256]{1,0:T(4,128)} %param.15) | copy-start | bytes 12292
  46.7 8.5 %copy-start.10 = (f32[4,2048]{1,0:T(4,128)S(1)}, f32[4,2048]{1,0:T(4,128)}, u32[]{:S(2)}) copy-start(f32[4,2048]{1,0:T(4,128)} %param.16) | copy-start | bytes 98308
  46.8 8.5 %copy-start.11 = (f32[4,2048]{1,0:T(4,128)S(1)}, f32[4,2048]{1,0:T(4,128)}, u32[]{:S(2)}) copy-start(f32[4,2048]{1,0:T(4,128)} %param.20) | copy-start | bytes 98308
  165.2 6.7 %copy-start.14 = (f32[2048]{0:T(1024)S(1)}, f32[2048]{0:T(1024)}, u32[]{:S(2)}) copy-start(f32[2048]{0:T(1024)} %get-tuple-element.75) | copy-start | bytes 24580
  165.2 6.7 %copy-start.7 = (f32[2048,256]{1,0:T(8,128)S(1)}, f32[2048,256]{1,0:T(8,128)}, u32[]{:S(2)}) copy-start(f32[2048,256]{1,0:T(8,128)} %get-tuple-element.156) | copy-start | bytes 6291460
  168.8 4.4 %copy-start.13 = (f32[2048]{0:T(1024)S(1)}, f32[2048]{0:T(1024)}, u32[]{:S(2)}) copy-start(f32[2048]{0:T(1024)} %get-tuple-element.76) | copy-start | bytes 24580
  168.8 4.4 %copy-start.4 = (f32[2048,256]{1,0:T(8,128)S(1)}, f32[2048,256]{1,0:T(8,128)}, u32[]{:S(2)}) copy-start(f32[2048,256]{1,0:T(8,128)} %get-tuple-element.157) | copy-start | bytes 6291460
  171.8 2.7 %copy-start.12 = (f32[2048]{0:T(1024)S(1)}, f32[2048]{0:T(1024)}, u32[]{:S(2)}) copy-start(f32[2048]{0:T(1024)} %get-tuple-element.77) | copy-start | bytes 24580
  171.8 2.7 %copy-start.5 = (f32[2048,256]{1,0:T(8,128)S(1)}, f32[2048,256]{1,0:T(8,128)}, u32[]{:S(2)}) copy-start(f32[2048,256]{1,0:T(8,128)} %get-tuple-element.158) | copy-start | bytes 6291460
  173.2 2.7 %copy-start.2 = (f32[256,2048]{1,0:T(8,128)S(1)}, f32[256,2048]{1,0:T(8,128)}, u32[]{:S(2)}) copy-start(f32[256,2048]{1,0:T(8,128)} %get-tuple-element.151) | copy-start | bytes 6291460
  174.5 3.0 %copy-start.6 = (f32[256,2048]{1,0:T(8,128)S(1)}, f32[256,2048]{1,0:T(8,128)}, u32[]{:S(2)}) copy-start(f32[256,2048]{1,0:T(8,128)} %get-tuple-element.152) | copy-start | bytes 6291460
  177.5 3.4 %copy-start = (f32[256,2048]{1,0:T(8,128)S(1)}, f32[256,2048]{1,0:T(8,128)}, u32[]{:S(2)}) copy-start(f32[256,2048]{1,0:T(8,128)} %get-tuple-element.154) | copy-start | bytes 6291460
  239.4 5.4 %copy-start.1 = (f32[256,2048]{1,0:T(8,128)S(1)}, f32[256,2048]{1,0:T(8,128)}, u32[]{:S(2)}) copy-start(f32[256,2048]{1,0:T(8,128)} %get-tuple-element.154) | copy-start | bytes 6291460
  239.4 5.9 %copy-start.3 = (f32[256,2048]{1,0:T(8,128)S(1)}, f32[256,2048]{1,0:T(8,128)}, u32[]{:S(2)}) copy-start(f32[256,2048]{1,0:T(8,128)} %get-tuple-element.151) | copy-start | bytes 6291460
  245.3 4.5 %copy-start.9 = (f32[1,256,2048]{2,1,0:T(8,128)S(1)}, f32[1,256,2048]{2,1,0:T(8,128)}, u32[]{:S(2)}) copy-start(f32[1,256,2048]{2,1,0:T(8,128)} %fusion.35) | copy-start | bytes 6291460
  249.8 3.7 %copy-start.8 = (f32[1,2048,256]{2,1,0:T(8,128)S(1)}, f32[1,2048,256]{2,1,0:T(8,128)}, u32[]{:S(2)}) copy-start(f32[1,2048,256]{2,1,0:T(8,128)} %fusion.27) | copy-start | bytes 6291460
Sparse Core Ops, SparseCore 0:
  41.2 35.0 all-reduce.5
where the time goes:
time: 267 us; the launch traced here: 265 us
  blocking collectives  101 us (38%)
  other arithmetic  67.4 us (25%)
  between operations  56 us (21%)
  matrix products  32.6 us (12%)
  local copies, waits for them, and re-layouts  7.5 us (3%)
    psum x1, blocking collectives, update_block(): scalar_sum = lax.psum(scalars, BOTH_AXES)  42 us
    psum x1, blocking collectives, update_block(): upd_sq = lax.psum(jnp.sum(update * update), BOTH_AXES)  37.7 us
    dot_general x8, matrix products, update_block(): lax.dot_general(x_blk, dy_blk, (((0,), (0,)), ((), ())), preferred_elemen...  32.6 us
    another operation x10, other arithmetic, local_step(): jnp.stack([res_item[out_idx] for res_item in results])  27.1 us
    psum x1, blocking collectives, update_block(): row_sum = lax.psum(row_part, cols_axis)  21.3 us
    reduce_sum x8, other arithmetic, update_block(): upd_sq = lax.psum(jnp.sum(update * update), BOTH_AXES)  13.6 us
    another operation x8, other arithmetic, update_block(): jnp.stack([jnp.sum(row_part), jnp.sum(w_blk * w_blk), lead_col * jnp.sum(...  10.6 us
    reduce_sum x2, other arithmetic, update_block(): jnp.sum(w_blk * w_blk)  9.7 us
  transfers between devices with their start and end apart: 1, of which 0 were waited for; matrix products, arithmetic and copies ran while one was open for 11% of the time, Pallas kernels for 0%

commit v1 on v0

v1 whole, which is shorter than its diff:
```python
import functools

import jax
import jax.numpy as jnp
from jax import lax
from jax.experimental import pallas as pl
from jax.experimental.pallas import tpu as pltpu
from jax.sharding import PartitionSpec as P

EPS_ONE = 1e-30
EPS_TWO = 1e-3
F32 = jnp.float32
BF16 = jnp.bfloat16
MESH = pl.DeviceIdType.MESH
LOOKAHEAD = 3
SLOTS = 4
GRANT = 24 * 2**20


def stats_kernel(dims, hp_hbm, w_in, x_in, dy_in, row_in, col_in, w_out, x_out, dy_out, row_out, col_out,
                 g_ref, wi_ref, wo_ref, sa_ref, sb_ref, fac_ref, na_ref, nb_ref,
                 hp_ref, small_ref, big_ref, xt_ref, acc_ref, rec_a, rec_b, rec_s, pay_ref,
                 old_ri, old_ci, old_ro, old_co,
                 load_sem, w_sem, old_sem, send_a, recv_a, send_b, recv_b, send_s, recv_s):
    n_col, n_row, layers, m_loc, n_loc, tokens, len_a, len_b = dims
    n_mat = 2 * layers
    n_dev = n_col * n_row
    my_col = lax.axis_index('col')
    my_row = lax.axis_index('row')
    me = my_col * n_row + my_row

    def load_copies(layer, part):
        slot = lax.rem(2 * layer + part, SLOTS)
        small = (x_in if part == 0 else dy_out).at[layer]
        big = (dy_in if part == 0 else x_out).at[layer]
        return (pltpu.make_async_copy(small, small_ref.at[slot], load_sem.at[slot, 0]),
                pltpu.make_async_copy(big, big_ref.at[slot], load_sem.at[slot, 1]))

    def w_copy(layer, part):
        if part == 0:
            return pltpu.make_async_copy(w_in.at[layer], wi_ref.at[layer], w_sem.at[layer, 0])
        return pltpu.make_async_copy(w_out.at[layer], wo_ref.at[layer], w_sem.at[layer, 1])

    def start_load(layer, part):
        for copy in load_copies(layer, part):
            copy.start()

    barrier = pltpu.get_barrier_semaphore()
    for idx in range(LOOKAHEAD):
        start_load(idx // 2, idx % 2)
    for step in range(1, n_dev):
        peer = lax.rem(me + step, n_dev)
        pl.semaphore_signal(barrier, inc=1, device_id=(peer // n_row, lax.rem(peer, n_row)), device_id_type=MESH)
    old_copies = [pltpu.make_async_copy(src, dst, old_sem.at[k]) for k, (src, dst) in enumerate(
        ((row_in, old_ri), (col_in, old_ci), (row_out, old_ro), (col_out, old_co), (hp_hbm, hp_ref)))]
    for copy in old_copies:
        copy.start()

    def a_copy(layer, step, sending):
        peer = lax.rem(my_col + step, n_col)
        slot = my_col if sending else lax.rem(my_col + n_col - step, n_col)
        return pltpu.make_async_remote_copy(
            rec_a.at[layer, slot], rec_a.at[layer, slot], send_a.at[layer, peer], recv_a.at[layer, slot],
            device_id=(peer, my_row), device_id_type=MESH)

    def b_copy(layer, step, sending):
        peer = lax.rem(my_row + step, n_row)
        slot = my_row if sending else lax.rem(my_row + n_row - step, n_row)
        return pltpu.make_async_remote_copy(
            rec_b.at[layer, slot], rec_b.at[layer, slot], send_b.at[layer, peer], recv_b.at[layer, slot],
            device_id=(my_col, peer), device_id_type=MESH)

    def s_copy(step, sending):
        peer = lax.rem(me + step, n_dev)
        slot = me if sending else lax.rem(me + n_dev - step, n_dev)
        return pltpu.make_async_remote_copy(
            rec_s.at[slot], rec_s.at[slot], send_s.at[peer], recv_s.at[slot],
            device_id=(peer // n_row, lax.rem(peer, n_row)), device_id_type=MESH)

    def ab_copies(layer, sending):
        return [b_copy(layer, step, sending) for step in range(1, n_row)] + [
            a_copy(layer, step, sending) for step in range(1, n_col)]

    def s_copies(sending):
        return [s_copy(step, sending) for step in range(1, n_dev)]

    lane = lax.broadcasted_iota(jnp.int32, (1, 128), 1)

    def put(section, mat, val):
        cols = pl.ds(128 * section, 128)
        pay_ref[:, cols] = jnp.where(lane == mat, val, pay_ref[:, cols])

    pay_ref[...] = jnp.zeros_like(pay_ref)

    def grad_part(layer, part):
        mat = 2 * layer + part
        slot = lax.rem(mat, SLOTS)
        for copy in load_copies(layer, part):
            copy.wait()
        xt_ref[...] = small_ref[slot].T
        for blk in range(n_loc // 256):
            cols = pl.ds(256 * blk, 256)
            grad = jnp.dot(xt_ref[...], big_ref[slot, :, cols], preferred_element_type=F32)
            g_ref[mat, :, cols] = grad
            sq = grad * grad
            rec_b[layer, my_row, :, pl.ds(n_loc * part + 256 * blk, 256)] = jnp.sum(sq, axis=0, keepdims=True)
            lanes = sq[:, :128] + sq[:, 128:]
            if blk == 0:
                acc_ref[...] = lanes
            else:
                acc_ref[...] += lanes
        rec_a[layer, my_col, :, pl.ds(m_loc * part, m_loc)] = jnp.sum(acc_ref[...].T, axis=0, keepdims=True)

    def stats_part(layer):
        beta = hp_ref[0]
        for copy in ab_copies(layer, False):
            copy.wait_recv()
        sum_a = rec_a[layer, 0]
        for idx in range(1, n_col):
            sum_a += rec_a[layer, idx]
        sum_b = rec_b[layer, 0]
        for idx in range(1, n_row):
            sum_b += rec_b[layer, idx]
        for part in range(2):
            mat = 2 * layer + part
            old_a = (old_ri if part == 0 else old_co)[pl.ds(layer, 1), :]
            old_b = (old_ci if part == 0 else old_ro)[pl.ds(layer, 1), :]
            part_a = sum_a[:, m_loc * part:m_loc * (part + 1)]
            part_b = sum_b[:, n_loc * part:n_loc * (part + 1)]
            new_a = beta * old_a + (1.0 - beta) * (part_a / len_b + EPS_ONE)
            new_b = beta * old_b + (1.0 - beta) * (part_b / len_a + EPS_ONE)
            na_ref[part, pl.ds(layer, 1), :] = new_a
            nb_ref[part, pl.ds(layer, 1), :] = new_b
            if part == 0:
                norm = jnp.sum(new_a, axis=1, keepdims=True) / m_loc
                scale_a = lax.rsqrt(new_a / norm)
                scale_b = lax.rsqrt(new_b)
            else:
                norm = jnp.sum(new_b, axis=1, keepdims=True) / n_loc
                scale_a = lax.rsqrt(new_a)
                scale_b = lax.rsqrt(new_b / norm)
            put(1, mat, norm)
            sb_ref[mat] = scale_b
            sa_ref[mat] = jnp.broadcast_to(scale_a, (128, m_loc)).T

        def body(idx, accs):
            part = idx // (m_loc // 64)
            mat = 2 * layer + part
            rows = pl.ds(pl.multiple_of(64 * lax.rem(idx, m_loc // 64), 64), 64)
            row_scale = sa_ref[mat, rows, :]
            total = jnp.zeros((64, 128), F32)
            for blk in range(n_loc // 128):
                cols = pl.ds(128 * blk, 128)
                upd = g_ref[mat, rows, cols] * row_scale * sb_ref[mat, :, cols]
                total += upd * upd
            return total

        for part in range(2):
            total = jnp.zeros((64, 128), F32)
            for idx in range(m_loc // 64):
                total += body(part * (m_loc // 64) + idx, None)
            one = jnp.sum(total, axis=0, keepdims=True)
            put(0, 2 * layer + part, jnp.sum(one, axis=1, keepdims=True))

    def w_part(layer, part):
        w_copy(layer, part).wait()
        ref = wi_ref if part == 0 else wo_ref
        rows_all, cols_all = ref.shape[1], ref.shape[2]

        def body(idx, total):
            rows = pl.ds(pl.multiple_of(idx * (rows_all // 8), 8), rows_all // 8)
            val = ref[layer, rows, :]
            sq = (val * val).reshape(rows_all // 64, 8, cols_all)
            sq = jnp.sum(sq, axis=0)
            for blk in range(cols_all // 128):
                total += sq[:, 128 * blk:128 * (blk + 1)]
            return total

        total = lax.fori_loop(0, 8, body, jnp.zeros((8, 128), F32))
        one = jnp.sum(total, axis=0, keepdims=True)
        put(2, 2 * layer + part, jnp.sum(one, axis=1, keepdims=True))

    def layer_body(layer, carry):
        for part in range(2):
            ahead = 2 * layer + part + LOOKAHEAD
            ahead_part = (part + LOOKAHEAD) % 2
            ahead_layer = (ahead - ahead_part) // 2
            grad_part(layer, part)

            @pl.when(ahead < n_mat)
            def _():
                start_load(ahead_layer, ahead_part)

            if part == 0:
                @pl.when(layer == layers - 2)
                def _():
                    for idx in range(layers):
                        w_copy(idx, 0).start()

                @pl.when(layer == layers - 1)
                def _():
                    for idx in range(layers):
                        w_copy(idx, 1).start()

        @pl.when(layer == 0)
        def _():
            pl.semaphore_wait(barrier, n_dev - 1)
            for copy in old_copies:
                copy.wait()

        for copy in ab_copies(layer, True):
            copy.start()

        @pl.when(layer > 0)
        def _():
            stats_part(layer - 1)

        return carry

    lax.fori_loop(0, layers, layer_body, 0)

    def w_body(layer, carry):
        w_part(layer, 0)
        w_part(layer, 1)
        return carry

    lax.fori_loop(0, layers, w_body, 0)
    stats_part(layers - 1)

    rec_s[me] = pay_ref[...]
    for copy in s_copies(True):
        copy.start()

    def drain(layer, carry):
        for copy in ab_copies(layer, True):
            copy.wait_send()
        return carry

    lax.fori_loop(0, layers, drain, 0)
    for copy in s_copies(False):
        copy.wait_recv()
    norm_sum = jnp.zeros((1, 128), F32)
    w_sum = jnp.zeros((1, 128), F32)
    for dev in range(n_dev):
        norm_sum += rec_s[dev, :, 128:256]
        w_sum += rec_s[dev, :, 256:384]
    used = lane < n_mat
    mean_s = norm_sum / n_dev
    upd_sum = jnp.zeros((1, 128), F32)
    for dev in range(n_dev):
        norm = jnp.where(used, rec_s[dev, :, 128:256], 1.0)
        upd_sum += rec_s[dev, :, 0:128] * (mean_s / norm)
    n_total = float(len_a * len_b)
    upd_rms = jnp.sqrt(upd_sum / n_total)
    w_rms = jnp.sqrt(w_sum / n_total)
    step_size = hp_ref[1] * jnp.maximum(EPS_TWO, w_rms) / jnp.maximum(1.0, upd_rms / hp_ref[2])
    norm = jnp.where(used, pay_ref[:, 128:256], 1.0)
    fac_ref[...] = step_size * jnp.sqrt(mean_s / norm)
    for copy in s_copies(True):
        copy.wait_send()


def update_kernel(dims, g_ref, wi_ref, wo_ref, sa_ref, sb_ref, fac_ref, na_ref, nb_ref,
                  w_in_new, row_in_new, col_in_new, w_out_new, row_out_new, col_out_new,
                  stage_i, stage_o, sem_i, sem_o, stat_sem):
    layers, m_loc, n_loc = dims
    stat_copies = [pltpu.make_async_copy(src, dst, stat_sem.at[k]) for k, (src, dst) in enumerate(
        ((na_ref.at[0], row_in_new), (nb_ref.at[0], col_in_new), (nb_ref.at[1], row_out_new), (na_ref.at[1], col_out_new)))]
    for copy in stat_copies:
        copy.start()
    lane = lax.broadcasted_iota(jnp.int32, (1, 128), 1)
    chunk_i = m_loc // 4
    chunk_o = n_loc // 4

    def factor(mat):
        return jnp.sum(jnp.where(lane == mat, fac_ref[...], 0.0), axis=1, keepdims=True)

    def copy_in(layer, idx, slot):
        return pltpu.make_async_copy(stage_i.at[slot], w_in_new.at[layer, pl.ds(chunk_i * idx, chunk_i)], sem_i.at[slot])

    def copy_out(layer, idx, slot):
        return pltpu.make_async_copy(stage_o.at[slot], w_out_new.at[layer, pl.ds(chunk_o * idx, chunk_o)], sem_o.at[slot])

    def body(layer, carry):
        mat = 2 * layer
        fac = factor(mat)
        for idx in range(4):
            slot = idx

            @pl.when(layer > 0)
            def _():
                copy_in(layer - 1, idx, slot).wait()

            rows = pl.ds(chunk_i * idx, chunk_i)
            row_scale = sa_ref[mat, rows, :] * fac
            for blk in range(n_loc // 128):
                cols = pl.ds(128 * blk, 128)
                upd = g_ref[mat, rows, cols] * row_scale * sb_ref[mat, :, cols]
                stage_i[slot, :, cols] = wi_ref[layer, rows, cols] - upd
            copy_in(layer, idx, slot).start()
        mat = 2 * layer + 1
        fac = factor(mat)
        for idx in range(4):
            slot = idx

            @pl.when(layer > 0)
            def _():
                copy_out(layer - 1, idx, slot).wait()

            for sub in range(m_loc // 128):
                rows = pl.ds(128 * sub, 128)
                row_scale = sa_ref[mat, rows, :] * fac
                for blk in range(chunk_o // 128):
                    cols = pl.ds(chunk_o * idx + 128 * blk, 128)
                    upd = g_ref[mat, rows, cols] * row_scale * sb_ref[mat, :, cols]
                    here = pl.ds(128 * blk, 128)
                    stage_o[slot, here, rows] = wo_ref[layer, cols, rows] - upd.T
            copy_out(layer, idx, slot).start()
        return carry

    lax.fori_loop(0, layers, body, 0)
    for idx in range(4):
        copy_in(layers - 1, idx, idx).wait()
        copy_out(layers - 1, idx, idx).wait()
    for copy in stat_copies:
        copy.wait()


def solution(mesh):
    n_col = mesh.shape['col']
    n_row = mesh.shape['row']
    n_dev = n_col * n_row
    tile_in = P(None, 'row', 'col')
    tile_out = P(None, 'col', 'row')
    lane_row = P(None, None, 'row')
    lane_col = P(None, None, 'col')
    vec_row = P(None, 'row')
    vec_col = P(None, 'col')

    def local_step(hyper_params, w_in, x_in, dy_in, row_in, col_in, w_out, x_out, dy_out, row_out, col_out):
        layers, m_loc, n_loc = w_in.shape
        tokens = x_in.shape[1]
        n_mat = 2 * layers
        len_a, len_b = m_loc * n_row, n_loc * n_col
        dims = (n_col, n_row, layers, m_loc, n_loc, tokens, len_a, len_b)
        hbm = pl.BlockSpec(memory_space=pl.ANY)
        vmem = pl.BlockSpec(memory_space=pltpu.VMEM)
        mid = pl.pallas_call(
            functools.partial(stats_kernel, dims),
            out_shape=[
                pltpu.VMEM((n_mat, m_loc, n_loc), F32),
                pltpu.VMEM((layers, m_loc, n_loc), F32),
                pltpu.VMEM((layers, n_loc, m_loc), F32),
                pltpu.VMEM((n_mat, m_loc, 128), F32),
                pltpu.VMEM((n_mat, 1, n_loc), F32),
                pltpu.VMEM((1, 128), F32),
                pltpu.VMEM((2, layers, m_loc), F32),
                pltpu.VMEM((2, layers, n_loc), F32),
            ],
            in_specs=[hbm] * 11,
            out_specs=[vmem] * 8,
            scratch_shapes=[
                pltpu.SMEM((3,), F32),
                pltpu.VMEM((SLOTS, tokens, m_loc), BF16),
                pltpu.VMEM((SLOTS, tokens, n_loc), BF16),
                pltpu.VMEM((m_loc, tokens), BF16),
                pltpu.VMEM((m_loc, 128), F32),
                pltpu.VMEM((layers, n_col, 1, 2 * m_loc), F32),
                pltpu.VMEM((layers, n_row, 1, 2 * n_loc), F32),
                pltpu.VMEM((n_dev, 1, 384), F32),
                pltpu.VMEM((1, 384), F32),
                pltpu.VMEM((layers, m_loc), F32),
                pltpu.VMEM((layers, n_loc), F32),
                pltpu.VMEM((layers, n_loc), F32),
                pltpu.VMEM((layers, m_loc), F32),
                pltpu.SemaphoreType.DMA((SLOTS, 2)),
                pltpu.SemaphoreType.DMA((layers, 2)),
                pltpu.SemaphoreType.DMA((5,)),
                pltpu.SemaphoreType.DMA((layers, n_col)),
                pltpu.SemaphoreType.DMA((layers, n_col)),
                pltpu.SemaphoreType.DMA((layers, n_row)),
                pltpu.SemaphoreType.DMA((layers, n_row)),
                pltpu.SemaphoreType.DMA((n_dev,)),
                pltpu.SemaphoreType.DMA((n_dev,)),
            ],
            compiler_params=pltpu.CompilerParams(collective_id=0, has_side_effects=True, vmem_limit_bytes=GRANT),
            name='adafactor_stats',
        )(*[pltpu.with_memory_space_constraint(item, pltpu.HBM) for item in (
            hyper_params, w_in, x_in, dy_in, row_in, col_in, w_out, x_out, dy_out, row_out, col_out)])
        mid = [pltpu.with_memory_space_constraint(item, pltpu.VMEM) for item in mid]
        out = pl.pallas_call(
            functools.partial(update_kernel, (layers, m_loc, n_loc)),
            out_shape=[
                jax.ShapeDtypeStruct(w_in.shape, F32),
                jax.ShapeDtypeStruct(row_in.shape, F32),
                jax.ShapeDtypeStruct(col_in.shape, F32),
                jax.ShapeDtypeStruct(w_out.shape, F32),
                jax.ShapeDtypeStruct(row_out.shape, F32),
                jax.ShapeDtypeStruct(col_out.shape, F32),
            ],
            in_specs=[vmem] * 8,
            out_specs=[hbm] * 6,
            scratch_shapes=[
                pltpu.VMEM((4, m_loc // 4, n_loc), F32),
                pltpu.VMEM((4, n_loc // 4, m_loc), F32),
                pltpu.SemaphoreType.DMA((4,)),
                pltpu.SemaphoreType.DMA((4,)),
                pltpu.SemaphoreType.DMA((4,)),
            ],
            compiler_params=pltpu.CompilerParams(vmem_limit_bytes=GRANT),
            name='adafactor_update',
        )(*mid)
        return tuple(out)

    return jax.shard_map(local_step, mesh=mesh, in_specs=(P(), tile_in, lane_row, lane_col, vec_row, vec_col, tile_out, lane_col, lane_row, vec_col, vec_row), out_specs=(tile_in, vec_row, vec_col, tile_out, vec_col, vec_row), check_vma=False)
```

time: 267 us -> 38.8 us (0.15)
  blocking collectives: 101 us -> 0 us
  other arithmetic: 67.4 us -> 0 us
  between operations: 56 us -> 0.64 us
  Pallas kernels: 0 us -> 38 us
  matrix products: 32.6 us -> 0 us
  local copies, waits for them, and re-layouts: 7.5 us -> 0 us
    psum x3 -> x0, blocking collectives: 101 us -> none  [the longest x1 42 us: update_block(): scalar_sum = lax.psum(scalars, BOTH_AXES)]
    pallas_call x0 -> x2, Pallas kernels: none -> 38 us  [the longest x1 32 us: local_step(): pl.pallas_call(functools.partial(stats_kernel, dims), out_shape=[pltpu.VM...]
    another operation x18 -> x0, other arithmetic: 37.7 us -> none  [the longest x10 27.1 us: local_step(): jnp.stack([res_item[out_idx] for res_item in results])]
    dot_general x8 -> x0, matrix products: 32.6 us -> none  [update_block(): lax.dot_general(x_blk, dy_blk, (((0,), (0,)), ((), ())), preferred_elemen...]
    reduce_sum x10 -> x0, other arithmetic: 23.3 us -> none  [the longest x8 13.6 us: update_block(): upd_sq = lax.psum(jnp.sum(update * update), BOTH_AXES)]
    slice x9 -> x0, local copies, waits for them, and re-layouts: 5.67 us -> none  [the longest x7 4.46 us: update_block(): w_rms = jnp.sqrt(scalar_sum[1] / n_total)]
    add x8 -> x0, other arithmetic: 2.97 us -> none  [update_block(): col_new = beta_two * col_old + (1.0 - beta_two) * (col_sum / n_rows)]
  transfers between devices with their start and end apart: 1 -> 0, of which waited for: 0 -> 0; matrix products, arithmetic and copies ran while one was open for 11% -> 0% of each run, Pallas kernels for 0% -> 0%
where the time goes in v1:
time: 38.8 us; the launch traced here: 38.7 us
  Pallas kernels  38 us (98%)
  between operations  0.64 us (2%)
    pallas_call x1, Pallas kernels, local_step(): pl.pallas_call(functools.partial(stats_kernel, dims), out_shape=[pltpu.VM...  32 us
    pallas_call x1, Pallas kernels, local_step(): pl.pallas_call(functools.partial(update_kernel, (layers, m_loc, n_loc)),...  6.06 us

profile of v1, /device:TPU:0, one launch (start us, length us, event | category | flops | bytes accessed | tf_op | source)
XLA Modules:
  0.0 38.7 jit_solution(3455700986540685545)
XLA Ops:
  0.6 32.0 %adafactor_stats.1 = (f32[8,256,2048]{2,1,0:T(8,128)S(1)}, f32[4,256,2048]{2,1,0:T(8,128)S(1)}, f32[4,2048,256]{2,1,0:T(8,128)S(1)}, f32[8,256,128]{2,1,0:T(8,12...) custom-call(f32[3]{0:T(128)} %hp_hbm.1, ...), custom_call_target="tpu_custom_call" | custom-call | tf_op jit(solution)/shard_map/adafactor_stats/pallas_call | solution.py:348
  32.6 6.1 %adafactor_update.1 = (f32[4,256,2048]{2,1,0:T(8,128)}, f32[4,256]{1,0:T(4,128)}, f32[4,2048]{1,0:T(4,128)}, f32[4,2048,256]{2,1,0:T(8,128)}, f32[4,2048]{1,0:T(4,128)}, /*index=5*/f32[4,256]{1,0:T(4,128)}) custom-call(f32[8,256,2048]{2,1,0:T(8,128)S(1)} %get-tuple-element.14.g_ref, f32[4,256,2048]{2,1,0:T(8,128)S(1)} %get-tuple-element.15.wi_ref, ...), custom_call_target="tpu_custom_call" | custom-call | tf_op jit(solution)/shard_map/adafactor_update/pallas_call | solution.py:391

commit v2 on v0

v2 whole, which is shorter than its diff:
```python
import functools

import jax
import jax.numpy as jnp
from jax import lax
from jax.experimental import pallas as pl
from jax.experimental.pallas import tpu as pltpu
from jax.sharding import PartitionSpec as P

EPS_ONE = 1e-30
EPS_TWO = 1e-3
F32 = jnp.float32
BF16 = jnp.bfloat16
MESH = pl.DeviceIdType.MESH
LOOKAHEAD = 3
SLOTS = 4
FIRST = 4
LATE = 5
T_SCALE = 2.0 ** -16
GRANT = 24 * 2**20


def stats_kernel(dims, hp_hbm, w_in, x_in, dy_in, row_in, col_in, w_out, x_out, dy_out, row_out, col_out,
                 gi_ref, go_ref, wi_ref, wo_ref, sa_ref, sb_ref, fac_ref, na_ref, nb_ref,
                 hp_ref, small_ref, big_ref, xt_ref, acc_ref, rec_a, rec_b, rec_s, pay_ref,
                 old_ri, old_ci, old_ro, old_co,
                 small_sem, big_sem, first_sem, w_sem, old_sem, send_a, recv_a, send_b, recv_b, send_s, recv_s):
    n_col, n_row, layers, m_loc, n_loc, tokens, len_a, len_b = dims
    n_mat = 2 * layers
    n_dev = n_col * n_row
    my_col = lax.axis_index('col')
    my_row = lax.axis_index('row')
    me = my_col * n_row + my_row
    first_cols = n_loc // FIRST

    def small_copy(mat):
        src = (dy_out if mat % 2 else x_in).at[mat // 2]
        return pltpu.make_async_copy(src, small_ref.at[mat % SLOTS], small_sem.at[mat % SLOTS])

    def big_copy(mat):
        src = (x_out if mat % 2 else dy_in).at[mat // 2]
        return pltpu.make_async_copy(src, big_ref.at[mat % SLOTS], big_sem.at[mat % SLOTS])

    def first_copy(idx):
        cols = pl.ds(first_cols * idx, first_cols)
        return pltpu.make_async_copy(dy_in.at[0, :, cols], big_ref.at[0, :, cols], first_sem.at[idx])

    def w_copy(mat):
        src, dst = (w_out, wo_ref) if mat % 2 else (w_in, wi_ref)
        return pltpu.make_async_copy(src.at[mat // 2], dst.at[mat // 2], w_sem.at[mat])

    small_copy(0).start()
    first_copy(0).start()
    small_copy(1).start()
    for idx in range(1, FIRST):
        first_copy(idx).start()
    for mat in range(1, LOOKAHEAD):
        small_copy(mat + 1).start()
        big_copy(mat).start()
    old_copies = [pltpu.make_async_copy(src, dst, old_sem.at[k]) for k, (src, dst) in enumerate(
        ((row_in, old_ri), (col_in, old_ci), (row_out, old_ro), (col_out, old_co), (hp_hbm, hp_ref)))]
    for copy in old_copies:
        copy.start()
    barrier = pltpu.get_barrier_semaphore()
    for col in range(n_col):
        for row in range(n_row):
            pl.semaphore_signal(barrier, inc=1, device_id=(col, row), device_id_type=MESH)

    def a_send(mat, step):
        return pltpu.make_async_remote_copy(
            rec_a.at[mat, my_col], rec_a.at[mat, my_col], send_a.at[0], recv_a.at[mat],
            device_id=(lax.rem(my_col + step, n_col), my_row), device_id_type=MESH)

    def b_send(mat, step):
        return pltpu.make_async_remote_copy(
            rec_b.at[mat, my_row], rec_b.at[mat, my_row], send_b.at[0], recv_b.at[mat],
            device_id=(my_col, lax.rem(my_row + step, n_row)), device_id_type=MESH)

    def s_send(step):
        peer = lax.rem(me + step, n_dev)
        return pltpu.make_async_remote_copy(
            rec_s.at[me], rec_s.at[me], send_s.at[0], recv_s.at[0],
            device_id=(peer // n_row, lax.rem(peer, n_row)), device_id_type=MESH)

    def take(ref, sem):
        pltpu.make_async_copy(ref, ref, sem).wait()

    lane = lax.broadcasted_iota(jnp.int32, (1, 128), 1)

    def put(place, val):
        pay_ref[...] = jnp.where(lane == place, val, pay_ref[...])

    pay_ref[...] = jnp.zeros_like(pay_ref)

    def g_of(mat):
        return (go_ref if mat % 2 else gi_ref).at[mat // 2]

    def row_sums(mat):
        rec_a[mat, my_col] = jnp.sum(acc_ref[mat % 2].T, axis=0, keepdims=True)

    def transpose_small(mat):
        xt_ref[mat % 2] = small_ref[mat % SLOTS].T

    def stats_scales(mat):
        beta = hp_ref[0]
        sum_a = rec_a[mat, 0]
        for idx in range(1, n_col):
            sum_a += rec_a[mat, idx]
        sum_b = rec_b[mat, 0]
        for idx in range(1, n_row):
            sum_b += rec_b[mat, idx]
        part, layer = mat % 2, mat // 2
        old_a = (old_co if part else old_ri)[pl.ds(layer, 1), :]
        old_b = (old_ro if part else old_ci)[pl.ds(layer, 1), :]
        new_a = beta * old_a + (1.0 - beta) * (sum_a / len_b + EPS_ONE)
        new_b = beta * old_b + (1.0 - beta) * (sum_b / len_a + EPS_ONE)
        na_ref[part, pl.ds(layer, 1), :] = new_a
        nb_ref[part, pl.ds(layer, 1), :] = new_b
        if part:
            norm = jnp.sum(new_b, axis=1, keepdims=True) / n_loc
            scale_a = lax.rsqrt(new_a)
            scale_b = lax.rsqrt(new_b / norm)
        else:
            norm = jnp.sum(new_a, axis=1, keepdims=True) / m_loc
            scale_a = lax.rsqrt(new_a / norm)
            scale_b = lax.rsqrt(new_b)
        sb_ref[mat] = scale_b
        sa_ref[mat] = jnp.broadcast_to(scale_a, (128, m_loc)).T
        return norm

    def square_piece(mat, idx, total):
        grad = g_of(mat)
        if mat % 2:
            for blk in range(n_loc // 128 // 8):
                cols = pl.ds(n_loc // 8 * idx + 128 * blk, 128)
                acc = jnp.zeros((8, 128), F32)
                for sub in range(m_loc // 64):
                    rows = pl.ds(64 * sub, 64)
                    upd = grad[rows, cols] * sa_ref[mat, rows, :]
                    acc += jnp.sum((upd * upd).reshape(8, 8, 128), axis=0)
                scale = sb_ref[mat, :, cols]
                total += acc * (scale * scale)
        else:
            rows = pl.ds(m_loc // 8 * idx, m_loc // 8)
            acc = jnp.zeros((m_loc // 8, 128), F32)
            for blk in range(n_loc // 128):
                cols = pl.ds(128 * blk, 128)
                upd = grad[rows, cols] * sb_ref[mat, :, cols]
                acc += upd * upd
            scale = sa_ref[mat, rows, :]
            total += jnp.sum((acc * (scale * scale)).reshape(m_loc // 64, 8, 128), axis=0)
        return total

    def all_sum(tile):
        one = jnp.sum(tile, axis=0, keepdims=True)
        return jnp.sum(one, axis=1, keepdims=True)

    def square_done(mat, total, norm):
        put(mat, all_sum(total) * T_SCALE / norm)
        put(n_mat + mat, norm)

    def take_round(mat):
        take(rec_a.at[mat, pl.ds(0, n_col - 1)], recv_a.at[mat])
        take(rec_b.at[mat, pl.ds(0, n_row - 1)], recv_b.at[mat])

    def send_round(mat):
        for step in range(1, n_row):
            b_send(mat, step).start()
        for step in range(1, n_col):
            a_send(mat, step).start()

    def step(mat):
        with jax.named_scope(f'load_wait#m={mat}'):
            if mat == 0:
                small_copy(0).wait()
                transpose_small(0)
                first_copy(0).wait()
            else:
                big_copy(mat).wait()
                if mat + 1 < n_mat:
                    small_copy(mat + 1).wait()
        if mat + LOOKAHEAD + 1 < n_mat:
            small_copy(mat + LOOKAHEAD + 1).start()
        if mat + LOOKAHEAD < n_mat:
            big_copy(mat + LOOKAHEAD).start()
        if mat == n_mat - 2:
            w_copy(0).start()
        if mat == n_mat - 1:
            for idx in range(1, n_mat):
                w_copy(idx).start()
        if mat + 1 < n_mat and mat > 0:
            transpose_small(mat + 1)
        if mat > 0:
            row_sums(mat - 1)
        late = mat - LATE
        if late >= 0:
            with jax.named_scope(f'round_wait#m={late}'):
                take_round(late)
            norm = stats_scales(late)
            total = jnp.zeros((8, 128), F32)
        grad_ref = g_of(mat)
        for blk in range(n_loc // 256):
            if mat == 0 and blk and (256 * blk) % first_cols == 0:
                first_copy(256 * blk // first_cols).wait()
            cols = pl.ds(256 * blk, 256)
            grad = jnp.dot(xt_ref[mat % 2], big_ref[mat % SLOTS, :, cols], preferred_element_type=F32)
            grad_ref[:, cols] = grad
            sq = grad * grad
            rec_b[mat, my_row, :, cols] = jnp.sum(sq, axis=0, keepdims=True)
            lanes = sq[:, :128] + sq[:, 128:]
            if blk == 0:
                acc_ref[mat % 2] = lanes
            else:
                acc_ref[mat % 2] += lanes
            if late >= 0:
                total = square_piece(late, blk, total)
        if late >= 0:
            square_done(late, total, norm)
        if mat == 0:
            small_copy(1).wait()
            transpose_small(1)
        if mat == 1:
            with jax.named_scope('barrier_wait'):
                pl.semaphore_wait(barrier, n_dev)
        if mat > 0:
            send_round(mat - 1)

    for mat in range(n_mat):
        with jax.named_scope(f'step#m={mat}'):
            if mat == LATE:
                for copy in old_copies:
                    copy.wait()
            step(mat)
    last = n_mat - 1
    with jax.named_scope('last_send'):
        row_sums(last)
        send_round(last)

    with jax.named_scope('w_sums'):
        for mat in range(n_mat):
            late = mat + n_mat - LATE
            if late < last:
                with jax.named_scope(f'round_wait#m={late}'):
                    take_round(late)
                norm = stats_scales(late)
                total = jnp.zeros((8, 128), F32)
                for idx in range(8):
                    total = square_piece(late, idx, total)
                square_done(late, total, norm)
            with jax.named_scope(f'w_wait#m={mat}'):
                w_copy(mat).wait()
            ref = (wo_ref if mat % 2 else wi_ref).at[mat // 2]
            rows_all, cols_all = ref.shape
            total = jnp.zeros((8, 128), F32)
            for idx in range(8):
                val = ref[pl.ds(rows_all // 8 * idx, rows_all // 8), :]
                sq = jnp.sum((val * val).reshape(rows_all // 64, 8, cols_all), axis=0)
                for blk in range(cols_all // 128):
                    total += sq[:, 128 * blk:128 * (blk + 1)]
            put(2 * n_mat + mat, all_sum(total))

    with jax.named_scope('last_wait'):
        take_round(last)
    with jax.named_scope('last_stats'):
        norm = stats_scales(last)
        total = jnp.zeros((8, 128), F32)
        for idx in range(8):
            total = square_piece(last, idx, total)
        square_done(last, total, norm)

    with jax.named_scope('s_send'):
        rec_s[me] = pay_ref[...]
        for step_idx in range(1, n_dev):
            s_send(step_idx).start()
    take(rec_a.at[:, pl.ds(0, n_col - 1)], send_a.at[0])
    take(rec_b.at[:, pl.ds(0, n_row - 1)], send_b.at[0])
    with jax.named_scope('s_wait'):
        take(rec_s.at[pl.ds(0, n_dev - 1)], recv_s.at[0])
    parts = [rec_s[dev] for dev in range(n_dev)]
    while len(parts) > 1:
        parts = [parts[k] + parts[k + 1] for k in range(0, len(parts), 2)]
    total = parts[0]
    used = lane < n_mat
    mean_s = pltpu.roll(total, 128 - n_mat, 1) / n_dev
    w_sum = pltpu.roll(total, 128 - 2 * n_mat, 1)
    norm = jnp.where(used, pltpu.roll(pay_ref[...], 128 - n_mat, 1), 1.0)
    n_total = float(len_a * len_b)
    upd_rms = jnp.sqrt(total * mean_s / (T_SCALE * n_total))
    w_rms = jnp.sqrt(w_sum / n_total)
    step_size = hp_ref[1] * jnp.maximum(EPS_TWO, w_rms) / jnp.maximum(1.0, upd_rms / hp_ref[2])
    fac_ref[...] = jnp.where(used, step_size * jnp.sqrt(mean_s / norm), 0.0)
    take(rec_s.at[pl.ds(0, n_dev - 1)], send_s.at[0])


def update_kernel(dims, gi_ref, go_ref, wi_ref, wo_ref, sa_ref, sb_ref, fac_ref, na_ref, nb_ref,
                  w_in_new, row_in_new, col_in_new, w_out_new, row_out_new, col_out_new,
                  stage_i, stage_o, sem_i, sem_o, stat_sem):
    layers, m_loc, n_loc = dims
    stat_copies = [pltpu.make_async_copy(src, dst, stat_sem.at[k]) for k, (src, dst) in enumerate(
        ((na_ref.at[0], row_in_new), (nb_ref.at[0], col_in_new), (nb_ref.at[1], row_out_new), (na_ref.at[1], col_out_new)))]
    for copy in stat_copies:
        copy.start()
    lane = lax.broadcasted_iota(jnp.int32, (1, 128), 1)
    chunk_i = m_loc // 4
    chunk_o = n_loc // 4

    def factor(mat):
        return jnp.sum(jnp.where(lane == mat, fac_ref[...], 0.0), axis=1, keepdims=True)

    def copy_in(layer, idx, slot):
        return pltpu.make_async_copy(stage_i.at[slot], w_in_new.at[layer, pl.ds(chunk_i * idx, chunk_i)], sem_i.at[slot])

    def copy_out(layer, idx, slot):
        return pltpu.make_async_copy(stage_o.at[slot], w_out_new.at[layer, pl.ds(chunk_o * idx, chunk_o)], sem_o.at[slot])

    def body(layer, carry):
        mat = 2 * layer
        fac = factor(mat)
        for idx in range(4):
            slot = idx

            @pl.when(layer > 0)
            def _():
                copy_in(layer - 1, idx, slot).wait()

            rows = pl.ds(chunk_i * idx, chunk_i)
            row_scale = sa_ref[mat, rows, :] * fac
            for blk in range(n_loc // 128):
                cols = pl.ds(128 * blk, 128)
                upd = gi_ref[layer, rows, cols] * row_scale * sb_ref[mat, :, cols]
                stage_i[slot, :, cols] = wi_ref[layer, rows, cols] - upd
            copy_in(layer, idx, slot).start()
        mat = 2 * layer + 1
        fac = factor(mat)
        for idx in range(4):
            slot = idx

            @pl.when(layer > 0)
            def _():
                copy_out(layer - 1, idx, slot).wait()

            for sub in range(m_loc // 128):
                rows = pl.ds(128 * sub, 128)
                row_scale = sa_ref[mat, rows, :] * fac
                for blk in range(chunk_o // 128):
                    cols = pl.ds(chunk_o * idx + 128 * blk, 128)
                    upd = go_ref[layer, rows, cols] * row_scale * sb_ref[mat, :, cols]
                    here = pl.ds(128 * blk, 128)
                    stage_o[slot, here, rows] = wo_ref[layer, cols, rows] - upd.T
            copy_out(layer, idx, slot).start()
        return carry

    lax.fori_loop(0, layers, body, 0)
    for idx in range(4):
        copy_in(layers - 1, idx, idx).wait()
        copy_out(layers - 1, idx, idx).wait()
    for copy in stat_copies:
        copy.wait()


def solution(mesh):
    n_col = mesh.shape['col']
    n_row = mesh.shape['row']
    n_dev = n_col * n_row
    tile_in = P(None, 'row', 'col')
    tile_out = P(None, 'col', 'row')
    lane_row = P(None, None, 'row')
    lane_col = P(None, None, 'col')
    vec_row = P(None, 'row')
    vec_col = P(None, 'col')

    def local_step(hyper_params, w_in, x_in, dy_in, row_in, col_in, w_out, x_out, dy_out, row_out, col_out):
        layers, m_loc, n_loc = w_in.shape
        tokens = x_in.shape[1]
        n_mat = 2 * layers
        len_a, len_b = m_loc * n_row, n_loc * n_col
        dims = (n_col, n_row, layers, m_loc, n_loc, tokens, len_a, len_b)
        hbm = pl.BlockSpec(memory_space=pl.ANY)
        vmem = pl.BlockSpec(memory_space=pltpu.VMEM)
        mid = pl.pallas_call(
            functools.partial(stats_kernel, dims),
            out_shape=[
                pltpu.VMEM((layers, m_loc, n_loc), F32),
                pltpu.VMEM((layers, m_loc, n_loc), F32),
                pltpu.VMEM((layers, m_loc, n_loc), F32),
                pltpu.VMEM((layers, n_loc, m_loc), F32),
                pltpu.VMEM((n_mat, m_loc, 128), F32),
                pltpu.VMEM((n_mat, 1, n_loc), F32),
                pltpu.VMEM((1, 128), F32),
                pltpu.VMEM((2, layers, m_loc), F32),
                pltpu.VMEM((2, layers, n_loc), F32),
            ],
            in_specs=[hbm] * 11,
            out_specs=[vmem] * 9,
            scratch_shapes=[
                pltpu.SMEM((3,), F32),
                pltpu.VMEM((SLOTS, tokens, m_loc), BF16),
                pltpu.VMEM((SLOTS, tokens, n_loc), BF16),
                pltpu.VMEM((2, m_loc, tokens), BF16),
                pltpu.VMEM((2, m_loc, 128), F32),
                pltpu.VMEM((n_mat, n_col, 1, m_loc), F32),
                pltpu.VMEM((n_mat, n_row, 1, n_loc), F32),
                pltpu.VMEM((n_dev, 1, 128), F32),
                pltpu.VMEM((1, 128), F32),
                pltpu.VMEM((layers, m_loc), F32),
                pltpu.VMEM((layers, n_loc), F32),
                pltpu.VMEM((layers, n_loc), F32),
                pltpu.VMEM((layers, m_loc), F32),
                pltpu.SemaphoreType.DMA((SLOTS,)),
                pltpu.SemaphoreType.DMA((SLOTS,)),
                pltpu.SemaphoreType.DMA((FIRST,)),
                pltpu.SemaphoreType.DMA((n_mat,)),
                pltpu.SemaphoreType.DMA((5,)),
                pltpu.SemaphoreType.DMA((1,)),
                pltpu.SemaphoreType.DMA((n_mat,)),
                pltpu.SemaphoreType.DMA((1,)),
                pltpu.SemaphoreType.DMA((n_mat,)),
                pltpu.SemaphoreType.DMA((1,)),
                pltpu.SemaphoreType.DMA((1,)),
            ],
            compiler_params=pltpu.CompilerParams(collective_id=0, has_side_effects=True, vmem_limit_bytes=GRANT),
            name='adafactor_stats',
        )(*[pltpu.with_memory_space_constraint(item, pltpu.HBM) for item in (
            hyper_params, w_in, x_in, dy_in, row_in, col_in, w_out, x_out, dy_out, row_out, col_out)])
        mid = [pltpu.with_memory_space_constraint(item, pltpu.VMEM) for item in mid]
        out = pl.pallas_call(
            functools.partial(update_kernel, (layers, m_loc, n_loc)),
            out_shape=[
                jax.ShapeDtypeStruct(w_in.shape, F32),
                jax.ShapeDtypeStruct(row_in.shape, F32),
                jax.ShapeDtypeStruct(col_in.shape, F32),
                jax.ShapeDtypeStruct(w_out.shape, F32),
                jax.ShapeDtypeStruct(row_out.shape, F32),
                jax.ShapeDtypeStruct(col_out.shape, F32),
            ],
            in_specs=[vmem] * 9,
            out_specs=[hbm] * 6,
            scratch_shapes=[
                pltpu.VMEM((4, m_loc // 4, n_loc), F32),
                pltpu.VMEM((4, n_loc // 4, m_loc), F32),
                pltpu.SemaphoreType.DMA((4,)),
                pltpu.SemaphoreType.DMA((4,)),
                pltpu.SemaphoreType.DMA((4,)),
            ],
            compiler_params=pltpu.CompilerParams(vmem_limit_bytes=GRANT),
            name='adafactor_update',
        )(*mid)
        return tuple(out)

    return jax.shard_map(local_step, mesh=mesh, in_specs=(P(), tile_in, lane_row, lane_col, vec_row, vec_col, tile_out, lane_col, lane_row, vec_col, vec_row), out_specs=(tile_in, vec_row, vec_col, tile_out, vec_col, vec_row), check_vma=False)
```

time: 267 us -> 35.9 us (0.13)
  blocking collectives: 101 us -> 0 us
  other arithmetic: 67.4 us -> 0 us
  between operations: 56 us -> 0.64 us
  Pallas kernels: 0 us -> 35.1 us
  matrix products: 32.6 us -> 0 us
  local copies, waits for them, and re-layouts: 7.5 us -> 0 us
    psum x3 -> x0, blocking collectives: 101 us -> none  [the longest x1 42 us: update_block(): scalar_sum = lax.psum(scalars, BOTH_AXES)]
    another operation x18 -> x0, other arithmetic: 37.7 us -> none  [the longest x10 27.1 us: local_step(): jnp.stack([res_item[out_idx] for res_item in results])]
    pallas_call x0 -> x2, Pallas kernels: none -> 35.1 us  [the longest x1 29 us: local_step(): pl.pallas_call(functools.partial(stats_kernel, dims), out_shape=[pltpu.VM...]
    dot_general x8 -> x0, matrix products: 32.6 us -> none  [update_block(): lax.dot_general(x_blk, dy_blk, (((0,), (0,)), ((), ())), preferred_elemen...]
    reduce_sum x10 -> x0, other arithmetic: 23.3 us -> none  [the longest x8 13.6 us: update_block(): upd_sq = lax.psum(jnp.sum(update * update), BOTH_AXES)]
    slice x9 -> x0, local copies, waits for them, and re-layouts: 5.67 us -> none  [the longest x7 4.46 us: update_block(): w_rms = jnp.sqrt(scalar_sum[1] / n_total)]
    add x8 -> x0, other arithmetic: 2.97 us -> none  [update_block(): col_new = beta_two * col_old + (1.0 - beta_two) * (col_sum / n_rows)]
  transfers between devices with their start and end apart: 1 -> 0, of which waited for: 0 -> 0; matrix products, arithmetic and copies ran while one was open for 11% -> 0% of each run, Pallas kernels for 0% -> 0%
where the time goes in v2:
time: 35.9 us; the launch traced here: 35.7 us
  Pallas kernels  35.1 us (98%)
  between operations  0.64 us (2%)
    pallas_call x1, Pallas kernels, local_step(): pl.pallas_call(functools.partial(stats_kernel, dims), out_shape=[pltpu.VM...  29 us
    pallas_call x1, Pallas kernels, local_step(): pl.pallas_call(functools.partial(update_kernel, (layers, m_loc, n_loc)),...  6.06 us

profile of v2, /device:TPU:0, one launch (start us, length us, event | category | flops | bytes accessed | tf_op | source)
XLA Modules:
  0.0 35.7 jit_solution(18117894864175001253)
XLA Ops:
  0.6 29.0 %adafactor_stats.1 = (f32[4,256,2048]{2,1,0:T(8,128)S(1)}, f32[4,256,2048]{2,1,0:T(8,128)S(1)}, f32[4,256,2048]{2,1,0:T(8,128)S(1)}, f32[4,2048,256]{2,1,0:T(8,1...) custom-call(f32[3]{0:T(128)} %hp_hbm.1, ...), custom_call_target="tpu_custom_call" | custom-call | tf_op jit(solution)/shard_map/adafactor_stats/pallas_call | solution.py:380
  29.7 6.1 %adafactor_update.1 = (f32[4,256,2048]{2,1,0:T(8,128)}, f32[4,256]{1,0:T(4,128)}, f32[4,2048]{1,0:T(4,128)}, f32[4,2048,256]{2,1,0:T(8,128)}, f32[4,2048]{1,0:T(4,128)}, /*index=5*/f32[4,256]{1,0:T(4,128)}) custom-call(f32[4,256,2048]{2,1,0:T(8,128)S(1)} %get-tuple-element.15.gi_ref, f32[4,256,2048]{2,1,0:T(8,128)S(1)} %get-tuple-element.16.go_ref, ...), custom_call_target="tpu_custom_call" | custom-call | tf_op jit(solution)/shard_map/adafactor_update/pallas_call | solution.py:426

commit v3 on v0

v3 whole, which is shorter than its diff:
```python
import functools

import jax
import jax.numpy as jnp
from jax import lax
from jax.experimental import pallas as pl
from jax.experimental.pallas import tpu as pltpu
from jax.sharding import PartitionSpec as P

EPS_ONE = 1e-30
EPS_TWO = 1e-3
F32 = jnp.float32
BF16 = jnp.bfloat16
MESH = pl.DeviceIdType.MESH
LOOKAHEAD = 2
SLOTS = 4
FIRST = 4
LATE = 4
CHUNKS = 8
T_SCALE = 2.0 ** -16
GRANT = 24 * 2**20


def stats_kernel(dims, hp_hbm, w_in, x_in, dy_in, row_in, col_in, w_out, x_out, dy_out, row_out, col_out,
                 gi_ref, go_ref, wi_ref, wo_ref, sa_ref, sb_ref, fac_ref, na_ref, nb_ref,
                 hp_ref, small_ref, big_ref, xt_ref, acc_ref, tot_ref, rec_a, rec_b, rec_s, pay_ref,
                 old_ri, old_ci, old_ro, old_co,
                 small_sem, big_sem, first_sem, w_sem, old_sem, send_sem, recv_a, recv_b, recv_s):
    n_col, n_row, layers, m_loc, n_loc, tokens, len_a, len_b = dims
    n_mat = 2 * layers
    n_dev = n_col * n_row
    my_col = lax.axis_index('col')
    my_row = lax.axis_index('row')
    me = my_col * n_row + my_row
    peer_col = [lax.rem(my_col + step, n_col) for step in range(n_col)]
    peer_row = [lax.rem(my_row + step, n_row) for step in range(n_row)]
    first_cols = n_loc // FIRST

    def small_copy(mat):
        src = (x_in if mat % 2 else dy_out).at[mat // 2]
        return pltpu.make_async_copy(src, small_ref.at[mat % SLOTS], small_sem.at[mat % SLOTS])

    def big_copy(mat):
        src = (dy_in if mat % 2 else x_out).at[mat // 2]
        return pltpu.make_async_copy(src, big_ref.at[mat % SLOTS], big_sem.at[mat % SLOTS])

    def first_copy(idx):
        cols = pl.ds(first_cols * idx, first_cols)
        return pltpu.make_async_copy(x_out.at[0, :, cols], big_ref.at[0, :, cols], first_sem.at[idx])

    def w_copy(mat):
        src, dst = (w_in, wi_ref) if mat % 2 else (w_out, wo_ref)
        return pltpu.make_async_copy(src.at[mat // 2], dst.at[mat // 2], w_sem.at[mat])

    small_copy(0).start()
    first_copy(0).start()
    barrier = pltpu.get_barrier_semaphore()
    for col in range(n_col):
        for row in range(n_row):
            pl.semaphore_signal(barrier, inc=1, device_id=(col, row), device_id_type=MESH)
    for idx in range(1, FIRST):
        first_copy(idx).start()
    small_copy(1).start()
    old_copies = [pltpu.make_async_copy(src, dst, old_sem.at[k]) for k, (src, dst) in enumerate(
        ((row_in, old_ri), (col_in, old_ci), (row_out, old_ro), (col_out, old_co), (hp_hbm, hp_ref)))]
    for copy in old_copies:
        copy.start()

    def send_round(mat):
        for step in range(1, n_col):
            pltpu.make_async_remote_copy(
                rec_a.at[mat, my_col], rec_a.at[mat, my_col], send_sem.at[0], recv_a.at[mat],
                device_id=(peer_col[step], my_row), device_id_type=MESH).start()
        for step in range(1, n_row):
            pltpu.make_async_remote_copy(
                rec_b.at[mat, my_row], rec_b.at[mat, my_row], send_sem.at[1], recv_b.at[mat],
                device_id=(my_col, peer_row[step]), device_id_type=MESH).start()

    def send_scalars():
        for col in reversed(range(n_col)):
            for row in range(n_row):
                if col or row:
                    pltpu.make_async_remote_copy(
                        rec_s.at[me], rec_s.at[me], send_sem.at[2], recv_s.at[0],
                        device_id=(peer_col[col], peer_row[row]), device_id_type=MESH).start()

    def take(ref, sem):
        pltpu.make_async_copy(ref, ref, sem).wait()

    def take_a(mat):
        take(rec_a.at[mat, pl.ds(0, n_col - 1)], recv_a.at[mat])

    def take_b(mat):
        take(rec_b.at[mat, pl.ds(0, n_row - 1)], recv_b.at[mat])

    lane = lax.broadcasted_iota(jnp.int32, (1, 128), 1)

    def put(place, val):
        pay_ref[...] = jnp.where(lane == place, val, pay_ref[...])

    pay_ref[...] = jnp.zeros_like(pay_ref)

    def g_of(mat):
        return (gi_ref if mat % 2 else go_ref).at[mat // 2]

    def row_sums(mat):
        rec_a[mat, my_col] = jnp.sum(acc_ref[mat % 2].T, axis=0, keepdims=True)

    def transpose_small(mat):
        xt_ref[mat % 2] = small_ref[mat % SLOTS].T

    def new_b(mat):
        beta = hp_ref[0]
        total = rec_b[mat, 0]
        for idx in range(1, n_row):
            total += rec_b[mat, idx]
        layer = mat // 2
        old = (old_ci if mat % 2 else old_ro)[pl.ds(layer, 1), :]
        new = beta * old + (1.0 - beta) * (total / len_a + EPS_ONE)
        nb_ref[mat % 2, pl.ds(layer, 1), :] = new
        sb_ref[mat] = lax.rsqrt(new)
        if mat % 2 == 0:
            put(n_mat + mat, jnp.sum(new, axis=1, keepdims=True) / n_loc)

    def square_piece(mat, idx):
        grad = g_of(mat)
        rows = pl.ds(m_loc // 8 * idx, m_loc // 8)
        acc = jnp.zeros((m_loc // 8, 128), F32)
        for blk in range(n_loc // 128):
            cols = pl.ds(128 * blk, 128)
            upd = grad[rows, cols] * sb_ref[mat, :, cols]
            acc += upd * upd
        tot_ref[mat, rows, :] = acc

    def new_a(mat):
        beta = hp_ref[0]
        total = rec_a[mat, 0]
        for idx in range(1, n_col):
            total += rec_a[mat, idx]
        layer = mat // 2
        old = (old_ri if mat % 2 else old_co)[pl.ds(layer, 1), :]
        new = beta * old + (1.0 - beta) * (total / len_b + EPS_ONE)
        na_ref[mat % 2, pl.ds(layer, 1), :] = new
        inv = lax.rsqrt(new)
        rows = jnp.sum(tot_ref[mat].T, axis=0, keepdims=True) * T_SCALE
        put(mat, jnp.sum(rows * (inv * inv), axis=1, keepdims=True))
        if mat % 2:
            put(n_mat + mat, jnp.sum(new, axis=1, keepdims=True) / m_loc)

    def scale_a(mat):
        new = na_ref[mat % 2, pl.ds(mat // 2, 1), :]
        sa_ref[mat] = jnp.broadcast_to(lax.rsqrt(new), (128, m_loc)).T

    def weight_sum(mat):
        ref = (wi_ref if mat % 2 else wo_ref).at[mat // 2]
        rows_all, cols_all = ref.shape
        total = jnp.zeros((8, 128), F32)
        for idx in range(8):
            val = ref[pl.ds(rows_all // 8 * idx, rows_all // 8), :]
            sq = jnp.sum((val * val).reshape(rows_all // 64, 8, cols_all), axis=0)
            for blk in range(cols_all // 128):
                total += sq[:, 128 * blk:128 * (blk + 1)]
        one = jnp.sum(total, axis=0, keepdims=True)
        put(2 * n_mat + mat, jnp.sum(one, axis=1, keepdims=True))

    def product_piece(mat, blk):
        cols = pl.ds(256 * blk, 256)
        grad = jnp.dot(xt_ref[mat % 2], big_ref[mat % SLOTS, :, cols], preferred_element_type=F32)
        g_of(mat)[:, cols] = grad
        sq = grad * grad
        rec_b[mat, my_row, :, cols] = jnp.sum(sq, axis=0, keepdims=True)
        lanes = sq[:, :128] + sq[:, 128:]
        if blk == 0:
            acc_ref[mat % 2] = lanes
        else:
            acc_ref[mat % 2] += lanes

    def load_ahead(mat):
        if mat < n_mat:
            big_copy(mat).start()
        if mat + 1 < n_mat:
            small_copy(mat + 1).start()

    last = n_mat - 1
    pieces = n_loc // 256
    for mat in range(n_mat):
        late = mat - LATE
        with jax.named_scope(f'step#m={mat}'):
            with jax.named_scope(f'wait#m={mat}'):
                if mat == 0:
                    small_copy(0).wait()
                    transpose_small(0)
                    first_copy(0).wait()
                    load_ahead(1)
                else:
                    big_copy(mat).wait()
                    load_ahead(mat + LOOKAHEAD)
                    if mat < last:
                        small_copy(mat + 1).wait()
                if mat == 1:
                    pl.semaphore_wait(barrier, n_dev)
                if late == 0:
                    for copy in old_copies:
                        copy.wait()
                if late >= 0:
                    take_b(late)
            if mat == last - 1:
                w_copy(0).start()
                w_copy(1).start()
            if mat == last:
                for idx in range(2, n_mat):
                    w_copy(idx).start()
            if mat > 0:
                row_sums(mat - 1)
                send_round(mat - 1)
                if mat < last:
                    transpose_small(mat + 1)
            if late >= 0:
                new_b(late)
            for blk in range(pieces):
                if mat == 0 and blk and (256 * blk) % first_cols == 0:
                    idx = 256 * blk // first_cols
                    first_copy(idx).wait()
                    if idx == FIRST // 2:
                        load_ahead(2)
                product_piece(mat, blk)
                if late >= 0:
                    square_piece(late, blk)
            if mat == 0:
                small_copy(1).wait()
                transpose_small(1)
    with jax.named_scope('last_send'):
        row_sums(last)
        send_round(last)

    left = [mat for mat in range(n_mat - LATE, last)]
    for mat in range(n_mat):
        with jax.named_scope(f'left#m={mat}'):
            with jax.named_scope(f'wait_left#m={mat}'):
                if mat < len(left):
                    take_b(left[mat])
                if mat < last:
                    take_a(mat)
                else:
                    take_b(last)
                w_copy(mat).wait()
            if mat < len(left):
                new_b(left[mat])
                for idx in range(8):
                    square_piece(left[mat], idx)
            if mat < last and mat not in left:
                new_a(mat)
            if mat == last:
                new_b(last)
                for idx in range(8):
                    square_piece(last, idx)
                for idx in left:
                    new_a(idx)
            weight_sum(mat)

    with jax.named_scope('last_wait'):
        take_a(last)
    with jax.named_scope('last_stats'):
        new_a(last)
    with jax.named_scope('s_send'):
        rec_s[me] = pay_ref[...]
        send_scalars()
    with jax.named_scope('scales'):
        for mat in range(n_mat):
            scale_a(mat)
        take(rec_a.at[:, pl.ds(0, n_col - 1)], send_sem.at[0])
        take(rec_b.at[:, pl.ds(0, n_row - 1)], send_sem.at[1])
        take(rec_s.at[pl.ds(0, n_dev - 1)], send_sem.at[2])
    with jax.named_scope('s_wait'):
        take(rec_s.at[pl.ds(0, n_dev - 1)], recv_s.at[0])
    parts = [rec_s[dev] for dev in range(n_dev)]
    while len(parts) > 1:
        parts = [parts[k] + parts[k + 1] for k in range(0, len(parts), 2)]
    total = parts[0]
    mean_s = pltpu.roll(total, 128 - n_mat, 1) / n_dev
    w_sum = pltpu.roll(total, 128 - 2 * n_mat, 1)
    n_total = float(len_a * len_b)
    upd_rms = jnp.sqrt(total * mean_s / (T_SCALE * n_total))
    w_rms = jnp.sqrt(w_sum / n_total)
    step_size = hp_ref[1] * jnp.maximum(EPS_TWO, w_rms) / jnp.maximum(1.0, upd_rms / hp_ref[2])
    fac_ref[...] = jnp.where(lane < n_mat, step_size * jnp.sqrt(mean_s), 0.0)


def update_kernel(dims, gi_ref, go_ref, wi_ref, wo_ref, sa_ref, sb_ref, fac_ref, na_ref, nb_ref,
                  w_in_new, row_in_new, col_in_new, w_out_new, row_out_new, col_out_new,
                  stage_i, stage_o, sem_i, sem_o, stat_sem):
    layers, m_loc, n_loc = dims
    lane = lax.broadcasted_iota(jnp.int32, (1, 128), 1)
    chunk_i = m_loc // CHUNKS
    chunk_o = n_loc // CHUNKS
    stat_copies = [pltpu.make_async_copy(src, dst, stat_sem.at[k]) for k, (src, dst) in enumerate(
        ((na_ref.at[1], row_in_new), (nb_ref.at[1], col_in_new), (nb_ref.at[0], row_out_new), (na_ref.at[0], col_out_new)))]

    def factor(mat):
        return jnp.sum(jnp.where(lane == mat, fac_ref[...], 0.0), axis=1, keepdims=True)

    def copy_in(layer, idx):
        return pltpu.make_async_copy(stage_i.at[idx], w_in_new.at[layer, pl.ds(chunk_i * idx, chunk_i)], sem_i.at[idx])

    def copy_out(layer, idx):
        return pltpu.make_async_copy(stage_o.at[idx], w_out_new.at[layer, pl.ds(chunk_o * idx, chunk_o)], sem_o.at[idx])

    def body(layer, carry):
        fac_i = factor(2 * layer + 1)
        fac_o = factor(2 * layer)
        for idx in range(CHUNKS):
            @pl.when(layer > 0)
            def _():
                copy_in(layer - 1, idx).wait()

            mat = 2 * layer + 1
            rows = pl.ds(chunk_i * idx, chunk_i)
            row_scale = sa_ref[mat, rows, :] * fac_i
            for blk in range(n_loc // 128):
                cols = pl.ds(128 * blk, 128)
                upd = gi_ref[layer, rows, cols] * row_scale * sb_ref[mat, :, cols]
                stage_i[idx, :, cols] = wi_ref[layer, rows, cols] - upd
            copy_in(layer, idx).start()

            @pl.when(layer > 0)
            def _():
                copy_out(layer - 1, idx).wait()

            mat = 2 * layer
            for sub in range(m_loc // 128):
                rows = pl.ds(128 * sub, 128)
                row_scale = sa_ref[mat, rows, :] * fac_o
                for blk in range(chunk_o // 128):
                    cols = pl.ds(chunk_o * idx + 128 * blk, 128)
                    upd = go_ref[layer, rows, cols] * row_scale * sb_ref[mat, :, cols]
                    stage_o[idx, pl.ds(128 * blk, 128), rows] = wo_ref[layer, cols, rows] - upd.T
            copy_out(layer, idx).start()
        return carry

    lax.fori_loop(0, layers, body, 0)
    for copy in stat_copies:
        copy.start()
    for idx in range(CHUNKS):
        copy_in(layers - 1, idx).wait()
        copy_out(layers - 1, idx).wait()
    for copy in stat_copies:
        copy.wait()


def solution(mesh):
    n_col = mesh.shape['col']
    n_row = mesh.shape['row']
    n_dev = n_col * n_row
    tile_in = P(None, 'row', 'col')
    tile_out = P(None, 'col', 'row')
    lane_row = P(None, None, 'row')
    lane_col = P(None, None, 'col')
    vec_row = P(None, 'row')
    vec_col = P(None, 'col')

    def local_step(hyper_params, w_in, x_in, dy_in, row_in, col_in, w_out, x_out, dy_out, row_out, col_out):
        layers, m_loc, n_loc = w_in.shape
        tokens = x_in.shape[1]
        n_mat = 2 * layers
        len_a, len_b = m_loc * n_row, n_loc * n_col
        dims = (n_col, n_row, layers, m_loc, n_loc, tokens, len_a, len_b)
        hbm = pl.BlockSpec(memory_space=pl.ANY)
        vmem = pl.BlockSpec(memory_space=pltpu.VMEM)
        mid = pl.pallas_call(
            functools.partial(stats_kernel, dims),
            out_shape=[
                pltpu.VMEM((layers, m_loc, n_loc), F32),
                pltpu.VMEM((layers, m_loc, n_loc), F32),
                pltpu.VMEM((layers, m_loc, n_loc), F32),
                pltpu.VMEM((layers, n_loc, m_loc), F32),
                pltpu.VMEM((n_mat, m_loc, 128), F32),
                pltpu.VMEM((n_mat, 1, n_loc), F32),
                pltpu.VMEM((1, 128), F32),
                pltpu.VMEM((2, layers, m_loc), F32),
                pltpu.VMEM((2, layers, n_loc), F32),
            ],
            in_specs=[hbm] * 11,
            out_specs=[vmem] * 9,
            scratch_shapes=[
                pltpu.SMEM((3,), F32),
                pltpu.VMEM((SLOTS, tokens, m_loc), BF16),
                pltpu.VMEM((SLOTS, tokens, n_loc), BF16),
                pltpu.VMEM((2, m_loc, tokens), BF16),
                pltpu.VMEM((2, m_loc, 128), F32),
                pltpu.VMEM((n_mat, m_loc, 128), F32),
                pltpu.VMEM((n_mat, n_col, 1, m_loc), F32),
                pltpu.VMEM((n_mat, n_row, 1, n_loc), F32),
                pltpu.VMEM((n_dev, 1, 128), F32),
                pltpu.VMEM((1, 128), F32),
                pltpu.VMEM((layers, m_loc), F32),
                pltpu.VMEM((layers, n_loc), F32),
                pltpu.VMEM((layers, n_loc), F32),
                pltpu.VMEM((layers, m_loc), F32),
                pltpu.SemaphoreType.DMA((SLOTS,)),
                pltpu.SemaphoreType.DMA((SLOTS,)),
                pltpu.SemaphoreType.DMA((FIRST,)),
                pltpu.SemaphoreType.DMA((n_mat,)),
                pltpu.SemaphoreType.DMA((5,)),
                pltpu.SemaphoreType.DMA((3,)),
                pltpu.SemaphoreType.DMA((n_mat,)),
                pltpu.SemaphoreType.DMA((n_mat,)),
                pltpu.SemaphoreType.DMA((1,)),
            ],
            compiler_params=pltpu.CompilerParams(collective_id=0, has_side_effects=True, vmem_limit_bytes=GRANT),
            name='adafactor_stats',
        )(*[pltpu.with_memory_space_constraint(item, pltpu.HBM) for item in (
            hyper_params, w_in, x_in, dy_in, row_in, col_in, w_out, x_out, dy_out, row_out, col_out)])
        mid = [pltpu.with_memory_space_constraint(item, pltpu.VMEM) for item in mid]
        out = pl.pallas_call(
            functools.partial(update_kernel, (layers, m_loc, n_loc)),
            out_shape=[
                jax.ShapeDtypeStruct(w_in.shape, F32),
                jax.ShapeDtypeStruct(row_in.shape, F32),
                jax.ShapeDtypeStruct(col_in.shape, F32),
                jax.ShapeDtypeStruct(w_out.shape, F32),
                jax.ShapeDtypeStruct(row_out.shape, F32),
                jax.ShapeDtypeStruct(col_out.shape, F32),
            ],
            in_specs=[vmem] * 9,
            out_specs=[hbm] * 6,
            scratch_shapes=[
                pltpu.VMEM((CHUNKS, m_loc // CHUNKS, n_loc), F32),
                pltpu.VMEM((CHUNKS, n_loc // CHUNKS, m_loc), F32),
                pltpu.SemaphoreType.DMA((CHUNKS,)),
                pltpu.SemaphoreType.DMA((CHUNKS,)),
                pltpu.SemaphoreType.DMA((4,)),
            ],
            compiler_params=pltpu.CompilerParams(vmem_limit_bytes=GRANT),
            name='adafactor_update',
        )(*mid)
        return tuple(out)

    return jax.shard_map(local_step, mesh=mesh, in_specs=(P(), tile_in, lane_row, lane_col, vec_row, vec_col, tile_out, lane_col, lane_row, vec_col, vec_row), out_specs=(tile_in, vec_row, vec_col, tile_out, vec_col, vec_row), check_vma=False)
```

time: 267 us -> 35.6 us (0.13)
  blocking collectives: 101 us -> 0 us
  other arithmetic: 67.4 us -> 0 us
  between operations: 56 us -> 0.64 us
  Pallas kernels: 0 us -> 34.8 us
  matrix products: 32.6 us -> 0 us
  local copies, waits for them, and re-layouts: 7.5 us -> 0 us
    psum x3 -> x0, blocking collectives: 101 us -> none  [the longest x1 42 us: update_block(): scalar_sum = lax.psum(scalars, BOTH_AXES)]
    another operation x18 -> x0, other arithmetic: 37.7 us -> none  [the longest x10 27.1 us: local_step(): jnp.stack([res_item[out_idx] for res_item in results])]
    pallas_call x0 -> x2, Pallas kernels: none -> 34.8 us  [the longest x1 28 us: local_step(): pl.pallas_call(functools.partial(stats_kernel, dims), out_shape=[pltpu.VM...]
    dot_general x8 -> x0, matrix products: 32.6 us -> none  [update_block(): lax.dot_general(x_blk, dy_blk, (((0,), (0,)), ((), ())), preferred_elemen...]
    reduce_sum x10 -> x0, other arithmetic: 23.3 us -> none  [the longest x8 13.6 us: update_block(): upd_sq = lax.psum(jnp.sum(update * update), BOTH_AXES)]
    slice x9 -> x0, local copies, waits for them, and re-layouts: 5.67 us -> none  [the longest x7 4.46 us: update_block(): w_rms = jnp.sqrt(scalar_sum[1] / n_total)]
    add x8 -> x0, other arithmetic: 2.97 us -> none  [update_block(): col_new = beta_two * col_old + (1.0 - beta_two) * (col_sum / n_rows)]
  transfers between devices with their start and end apart: 1 -> 0, of which waited for: 0 -> 0; matrix products, arithmetic and copies ran while one was open for 11% -> 0% of each run, Pallas kernels for 0% -> 0%
where the time goes in v3:
time: 35.6 us; the launch traced here: 35.4 us
  Pallas kernels  34.8 us (98%)
  between operations  0.64 us (2%)
    pallas_call x1, Pallas kernels, local_step(): pl.pallas_call(functools.partial(stats_kernel, dims), out_shape=[pltpu.VM...  28 us
    pallas_call x1, Pallas kernels, local_step(): pl.pallas_call(functools.partial(update_kernel, (layers, m_loc, n_loc)),...  6.8 us

profile of v3, /device:TPU:0, one launch (start us, length us, event | category | flops | bytes accessed | tf_op | source)
XLA Modules:
  0.0 35.4 jit_solution(2310649846914454438)
XLA Ops:
  0.6 28.0 %adafactor_stats.1 = (f32[4,256,2048]{2,1,0:T(8,128)S(1)}, f32[4,256,2048]{2,1,0:T(8,128)S(1)}, f32[4,256,2048]{2,1,0:T(8,128)S(1)}, f32[4,2048,256]{2,1,0:T(8,1...) custom-call(f32[3]{0:T(128)} %hp_hbm.1, ...), custom_call_target="tpu_custom_call" | custom-call | tf_op jit(solution)/shard_map/adafactor_stats/pallas_call | solution.py:369
  28.6 6.8 %adafactor_update.1 = (f32[4,256,2048]{2,1,0:T(8,128)}, f32[4,256]{1,0:T(4,128)}, f32[4,2048]{1,0:T(4,128)}, f32[4,2048,256]{2,1,0:T(8,128)}, f32[4,2048]{1,0:T(4,128)}, /*index=5*/f32[4,256]{1,0:T(4,128)}) custom-call(f32[4,256,2048]{2,1,0:T(8,128)S(1)} %get-tuple-element.15.gi_ref, f32[4,256,2048]{2,1,0:T(8,128)S(1)} %get-tuple-element.16.go_ref, ...), custom_call_target="tpu_custom_call" | custom-call | tf_op jit(solution)/shard_map/adafactor_update/pallas_call | solution.py:414
